TPU v7x, 32 devices: a whole 2x2x4 slice. The times are simulated.
32 devices in a mesh: expert: 8 (over z, y), helper: 4 (over x, core).
Axes of the slice: x: 2, y: 2, z: 4, core: 2. Of those that a mesh axis runs over, the one named last changes fastest.
Arguments:
- tokens: bfloat16 [32768, 768], P(('expert', 'helper')), may hold values from -6 to 6
- gate: float32 [32768], P(('expert', 'helper')), may hold values from 0.2 to 1
- expert_ids: int32 [32768, 1], P(('expert', 'helper')), may hold values from 0 to 31; in each aligned block of 1024 rows (0 to 1023, 1024 to 2047, ...) at most 48 rows name the same one
- backup_ids: int32 [32768, 1], P(('expert', 'helper')), may hold values from 0 to 31; in each aligned block of 1024 rows (0 to 1023, 1024 to 2047, ...) at most 48 rows name the same one
- capacity: int32 [32], replicated, may hold values from 2 to 48
- w_in: bfloat16 [32, 768, 3072], P('expert', None, 'helper'), may hold values from -0.21875 to 0.21875
- w_out: bfloat16 [32, 3072, 768], P('expert', 'helper'), may hold values from -0.109375 to 0.109375
Outputs:
- mixed: bfloat16 [32768, 768], P(('expert', 'helper'))
Inputs may be any that keep to these rules, and one draw needn't show every extreme that they name: `expert_ids`: in the rows of one device no expert is the first expert of more than 48 rows; some expert reaches 48. `backup_ids`: in the rows of one device no expert is the backup of more than 48 rows; some expert reaches 48.
All inputs are finite; a program needn't handle non-finite values.
Results may differ from a plain program's by a relative error of at most 0.0095.
Values may be sent and summed in bfloat16 or wider, within the bound.
A program may use at most 192 MiB of HBM per device.

v0:
```python
import jax
import jax.numpy as jnp
from jax import lax
from jax.sharding import PartitionSpec as P


def assign(first, backup, capacity, count, slot):
    columns = jnp.arange(count, dtype=jnp.int32)
    onehot = (first[:, None] == columns[None, :]).astype(jnp.int32)
    rank = jnp.sum((jnp.cumsum(onehot, axis=0) - onehot) * onehot, axis=1)
    limit = jnp.sum(onehot * capacity[None, :], axis=1)
    kept = rank < limit
    spill = (backup[:, None] == columns[None, :]).astype(jnp.int32) * (1 - kept.astype(jnp.int32))[
        :, None
    ]
    spill_rank = jnp.sum((jnp.cumsum(spill, axis=0) - spill) * spill, axis=1)
    final = jnp.where(kept, first, backup)
    slots = jnp.where(kept, rank, slot + spill_rank)
    return (slots, final)


def quarter_term(rows, weight_in, weight_out):
    hidden = jax.nn.relu(jnp.dot(rows, weight_in, preferred_element_type=jnp.float32)).astype(
        jnp.bfloat16
    )
    return jnp.dot(hidden, weight_out, preferred_element_type=jnp.float32)


def on_device(tokens, gate, expert_ids, backup_ids, capacity, w_in, w_out):
    held = w_in.shape[0]
    experts = held * lax.axis_size("expert")
    helpers = lax.axis_size("helper")
    slot = max(6, 3 * tokens.shape[0] // (2 * experts))
    slots, final = assign(expert_ids[:, 0], backup_ids[:, 0], capacity, experts, slot)
    buffer = (
        jnp.zeros((2 * slot, experts, tokens.shape[1]), jnp.bfloat16).at[slots, final].set(tokens)
    )
    arrived = lax.all_to_all(buffer, "expert", split_axis=1, concat_axis=0, tiled=True)
    whole_in, whole_out = (
        lax.all_gather(w_in, "helper", axis=2, tiled=True),
        lax.all_gather(w_out, "helper", axis=1, tiled=True),
    )
    width = whole_in.shape[2] // helpers
    outputs = []
    for expert in range(held):
        total = jnp.zeros((arrived.shape[0], arrived.shape[2]), jnp.float32)
        for quarter in range(helpers):
            part = quarter_term(
                arrived[:, expert],
                whole_in[expert, :, quarter * width : (quarter + 1) * width],
                whole_out[expert, quarter * width : (quarter + 1) * width, :],
            )
            total = total + part.astype(jnp.bfloat16).astype(jnp.float32)
        outputs.append(total.astype(jnp.bfloat16))
    result = jnp.stack(outputs, axis=1)
    returned = lax.all_to_all(result, "expert", split_axis=0, concat_axis=1, tiled=True)
    picked = returned[slots, final]
    return (gate[:, None] * picked.astype(jnp.float32)).astype(jnp.bfloat16)


def solution(mesh):
    placed = (
        P(("expert", "helper"), None),
        P(("expert", "helper")),
        P(("expert", "helper"), None),
        P(("expert", "helper"), None),
        P(),
        P("expert", None, "helper"),
        P("expert", "helper", None),
    )
    return jax.shard_map(
        on_device,
        mesh=mesh,
        in_specs=placed,
        out_specs=P(("expert", "helper"), None),
        check_vma=False,
    )
```

profile of v0, /device:TPU:0, one launch (start us, length us, event | category | flops | bytes accessed | tf_op | source)
XLA Modules:
  0.0 485.7 jit_solution(15206841944600603158)
XLA Ops:
  8.1 9.0 %reduce-window.14 = s32[32,8,128]{2,1,0:T(8,128)S(1)} reduce-window(s32[32,8,128]{2,1,0:T(8,128)S(1)} %fusion.10, s32[]{:T(128)} %constant.32.clone.1), window={size=1x1x128 pad=0_0x0_0x127_0}, to_apply=%region_0.0 | reduce-window | flops 4161536 | bytes 262148 | tf_op jit(solution)/shard_map/reduce-window
  17.7 9.0 %reduce-window.16 = s32[32,8,128]{2,1,0:T(8,128)S(1)} reduce-window(s32[32,8,128]{2,1,0:T(8,128)S(1)} %fusion.11, s32[]{:T(128)} %constant.32.clone.1), window={size=1x1x128 pad=0_0x0_0x127_0}, to_apply=%region_4.5 | reduce-window | flops 4161536 | bytes 262148 | tf_op jit(solution)/shard_map/reduce-window.2
  27.5 8.8 %scatter_custom_fusion = bf16[3072,768]{1,0:T(8,128)(2,1)} fusion(s32[1024]{0:T(1024)S(1)} %broadcast_select_fusion, bf16[1024,768]{1,0:T(8,128)(2,1)} %param.7, bf16[]{:T(256)} %constant.31.clone.1), kind=kCustom, calls=%fused_computation.5 | custom fusion | bytes 4719104
  36.3 5.0 %copy.25 = bf16[96,32,768]{2,0,1:T(8,128)(2,1)S(1)} copy(bf16[96,32,768]{2,1,0:T(8,128)(2,1)} %bitcast.248) | data formatting | bytes 9437184 | tf_op jit(solution)/shard_map/scatter | solution.py:36
  41.3 111.5 %all_to_all.36 = bf16[96,32,768]{2,0,1:T(8,128)(2,1)S(1)} all-to-all(bf16[96,32,768]{2,0,1:T(8,128)(2,1)S(1)} %copy.25), channel_id=1, replica_groups=mesh['expert'=8,'helper'=4] {'expert'}, dimensions={1} | all-to-all | bytes 9437184 | tf_op jit(solution)/shard_map/all_to_all | solution.py:38
  155.3 97.2 %all-gather.5.cloned.1.call-done = bf16[4,3072,768]{2,1,0:T(8,128)(2,1)} async-done(((bf16[4,768,768]{2,1,0:T(8,128)(2,1)}), bf16[4,3072,768]{2,1,0:T(8,128)(2,1)}) %all-gather.5.cloned.1.call-update) | async-done | bytes 18874384 | tf_op jit(solution)/shard_map/all_gather | solution.py:41
  256.6 5.1 %convolution_convert_fusion.1 = bf16[768,768]{1,0:T(8,128)(2,1)} fusion(bf16[4,3072,768]{2,1,0:T(8,128)(2,1)} %all-gather.5.cloned.1.call-done, bf16[4,768,3072]{2,1,0:T(8,128)(2,1)} %all-gather.3.cloned.1.call-done, bf16[768,4,768]{2,0,1:T(8,128)(2,1)} %bitcast.253), kind=kOutput, calls=%fused_computation.28 | convolution fusion | flops 1813708800 | bytes 4718592 | tf_op jit(solution)/shard_map/dot_general | solution.py:26
  261.7 5.1 %convolution_convert_fusion = bf16[768,768]{1,0:T(8,128)(2,1)} fusion(bf16[4,3072,768]{2,1,0:T(8,128)(2,1)} %all-gather.5.cloned.1.call-done, bf16[4,768,3072]{2,1,0:T(8,128)(2,1)} %all-gather.3.cloned.1.call-done, bf16[768,4,768]{2,0,1:T(8,128)(2,1)} %bitcast.254), kind=kOutput, calls=%fused_computation.27 | convolution fusion | flops 1813708800 | bytes 4718592 | tf_op jit(solution)/shard_map/dot_general | solution.py:26
  271.0 5.1 %convolution_convert_fusion.5 = bf16[768,768]{1,0:T(8,128)(2,1)} fusion(bf16[4,3072,768]{2,1,0:T(8,128)(2,1)} %all-gather.5.cloned.1.call-done, bf16[4,768,3072]{2,1,0:T(8,128)(2,1)} %all-gather.3.cloned.1.call-done, bf16[768,4,768]{2,0,1:T(8,128)(2,1)} %bitcast.256), kind=kOutput, calls=%fused_computation.32 | convolution fusion | flops 1813708800 | bytes 4718592 | tf_op jit(solution)/shard_map/dot_general | solution.py:26
  276.1 5.2 %convolution_convert_fusion.4 = bf16[768,768]{1,0:T(8,128)(2,1)} fusion(bf16[4,3072,768]{2,1,0:T(8,128)(2,1)} %all-gather.5.cloned.1.call-done, bf16[4,768,3072]{2,1,0:T(8,128)(2,1)} %all-gather.3.cloned.1.call-done, bf16[768,4,768]{2,0,1:T(8,128)(2,1)} %bitcast.257), kind=kOutput, calls=%fused_computation.31 | convolution fusion | flops 1813708800 | bytes 4718592 | tf_op jit(solution)/shard_map/dot_general | solution.py:26
  281.3 5.1 %convolution_convert_fusion.10 = bf16[768,768]{1,0:T(8,128)(2,1)} fusion(bf16[4,3072,768]{2,1,0:T(8,128)(2,1)} %all-gather.5.cloned.1.call-done, bf16[4,768,3072]{2,1,0:T(8,128)(2,1)} %all-gather.3.cloned.1.call-done, bf16[768,4,768]{2,0,1:T(8,128)(2,1)} %bitcast.258), kind=kOutput, calls=%fused_computation.37 | convolution fusion | flops 1813708800 | bytes 4718592 | tf_op jit(solution)/shard_map/dot_general | solution.py:26
  286.4 5.4 %convolution_convert_fusion.9 = bf16[768,768]{1,0:T(8,128)(2,1)} fusion(bf16[4,3072,768]{2,1,0:T(8,128)(2,1)} %all-gather.5.cloned.1.call-done, bf16[4,768,3072]{2,1,0:T(8,128)(2,1)} %all-gather.3.cloned.1.call-done, bf16[768,4,768]{2,0,1:T(8,128)(2,1)} %bitcast.259), kind=kOutput, calls=%fused_computation.36 | convolution fusion | flops 1813708800 | bytes 4718592 | tf_op jit(solution)/shard_map/dot_general | solution.py:26
  291.7 5.2 %convolution_convert_fusion.8 = bf16[768,768]{1,0:T(8,128)(2,1)} fusion(bf16[4,3072,768]{2,1,0:T(8,128)(2,1)} %all-gather.5.cloned.1.call-done, bf16[4,768,3072]{2,1,0:T(8,128)(2,1)} %all-gather.3.cloned.1.call-done, bf16[768,4,768]{2,0,1:T(8,128)(2,1)} %bitcast.260), kind=kOutput, calls=%fused_computation.35 | convolution fusion | flops 1813708800 | bytes 4718592 | tf_op jit(solution)/shard_map/dot_general | solution.py:26
  296.9 5.1 %convolution_convert_fusion.14 = bf16[768,768]{1,0:T(8,128)(2,1)} fusion(bf16[4,3072,768]{2,1,0:T(8,128)(2,1)} %all-gather.5.cloned.1.call-done, bf16[4,768,3072]{2,1,0:T(8,128)(2,1)} %all-gather.3.cloned.1.call-done, bf16[768,4,768]{2,0,1:T(8,128)(2,1)} %bitcast.261), kind=kOutput, calls=%fused_computation.41 | convolution fusion | flops 1813708800 | bytes 4718592 | tf_op jit(solution)/shard_map/dot_general | solution.py:26
  302.0 5.1 %convolution_convert_fusion.13 = bf16[768,768]{1,0:T(8,128)(2,1)} fusion(bf16[4,3072,768]{2,1,0:T(8,128)(2,1)} %all-gather.5.cloned.1.call-done, bf16[4,768,3072]{2,1,0:T(8,128)(2,1)} %all-gather.3.cloned.1.call-done, bf16[768,4,768]{2,0,1:T(8,128)(2,1)} %bitcast.262), kind=kOutput, calls=%fused_computation.40 | convolution fusion | flops 1813708800 | bytes 4718592 | tf_op jit(solution)/shard_map/dot_general | solution.py:26
  307.1 5.1 %convolution_convert_fusion.12 = bf16[768,768]{1,0:T(8,128)(2,1)} fusion(bf16[4,3072,768]{2,1,0:T(8,128)(2,1)} %all-gather.5.cloned.1.call-done, bf16[4,768,3072]{2,1,0:T(8,128)(2,1)} %all-gather.3.cloned.1.call-done, bf16[768,4,768]{2,0,1:T(8,128)(2,1)} %bitcast.263), kind=kOutput, calls=%fused_computation.39 | convolution fusion | flops 1813708800 | bytes 4718592 | tf_op jit(solution)/shard_map/dot_general | solution.py:26
  312.3 4.9 %fusion.5 = bf16[768,1,768]{2,0,1:T(8,128)(2,1)S(1)} fusion(bf16[768,768]{1,0:T(8,128)(2,1)} %convolution_convert_fusion, bf16[768,768]{1,0:T(8,128)(2,1)} %convolution_convert_fusion.1, bf16[768,768]{1,0:T(8,128)(2,1)S(1)} %convolution_convert_fusion.2, bf16[4,3072,768]{2,1,0:T(8,128)(2,1)} %all-gather.5.cloned.1.call-done, ...), kind=kOutput, calls=%fused_computation.46 | convolution fusion | flops 1818427392 | bytes 8257536 | tf_op jit(solution)/shard_map/dot_general | solution.py:26
  317.2 4.9 %fusion.4 = bf16[768,1,768]{2,0,1:T(8,128)(2,1)S(1)} fusion(bf16[768,768]{1,0:T(8,128)(2,1)} %convolution_convert_fusion.4, bf16[768,768]{1,0:T(8,128)(2,1)} %convolution_convert_fusion.5, bf16[768,768]{1,0:T(8,128)(2,1)S(1)} %convolution_convert_fusion.6, bf16[4,3072,768]{2,1,0:T(8,128)(2,1)} %all-gather.5.cloned.1.call-done, ...), kind=kOutput, calls=%fused_computation.45 | convolution fusion | flops 1818427392 | bytes 8257536 | tf_op jit(solution)/shard_map/dot_general | solution.py:26
  322.1 5.2 %fusion.3 = bf16[768,1,768]{2,0,1:T(8,128)(2,1)S(1)} fusion(bf16[768,768]{1,0:T(8,128)(2,1)} %convolution_convert_fusion.8, bf16[768,768]{1,0:T(8,128)(2,1)} %convolution_convert_fusion.9, bf16[768,768]{1,0:T(8,128)(2,1)} %convolution_convert_fusion.10, bf16[4,3072,768]{2,1,0:T(8,128)(2,1)} %all-gather.5.cloned.1.call-done, ...), kind=kOutput, calls=%fused_computation.44 | convolution fusion | flops 1818427392 | bytes 8257536 | tf_op jit(solution)/shard_map/dot_general | solution.py:26
  327.3 6.5 %fusion.2 = bf16[768,1,768]{2,0,1:T(8,128)(2,1)} fusion(bf16[768,768]{1,0:T(8,128)(2,1)} %convolution_convert_fusion.12, bf16[768,768]{1,0:T(8,128)(2,1)} %convolution_convert_fusion.13, bf16[768,768]{1,0:T(8,128)(2,1)} %convolution_convert_fusion.14, bf16[4,3072,768]{2,1,0:T(8,128)(2,1)} %all-gather.5.cloned.1.call-done, ...), kind=kOutput, calls=%fused_computation.43 | convolution fusion | flops 1818427392 | bytes 8257536 | tf_op jit(solution)/shard_map/dot_general | solution.py:26
  339.2 110.1 %all_to_all.37 = bf16[768,4,768]{2,1,0:T(4,128)(2,1)S(1)} all-to-all(bf16[768,4,768]{2,1,0:T(4,128)(2,1)S(1)} %copy.27), channel_id=1, replica_groups=mesh['expert'=8,'helper'=4] {'expert'}, dimensions={0} | all-to-all | bytes 9437184 | tf_op jit(solution)/shard_map/all_to_all | solution.py:56
  449.3 4.8 copy.34
  454.1 8.6 %all_to_all.33 = bf16[96,32,768]{2,1,0:T(8,128)(2,1)} reshape(bf16[96,8,4,768]{3,2,1,0:T(4,128)(2,1)} %bitcast.251) | data formatting | bytes 9437184 | tf_op jit(solution)/shard_map/all_to_all | solution.py:56
  462.7 14.3 %gather_fusion = bf16[1024,768]{1,0:T(8,128)(2,1)S(1)} fusion(bf16[96,32,768]{2,1,0:T(8,128)(2,1)} %all_to_all.33, s32[1024]{0:T(1024)S(1)} %bitcast.247), kind=kCustom, calls=%fused_computation | custom fusion | bytes 3153920 | tf_op jit(solution)/shard_map/gather | solution.py:57
  (45 shorter events, 20.2 us)
Async XLA Ops:
  6.5 148.8 %all-gather.3.cloned.1.call-start = ((), (), s32[]{:S(2)}) async-start(), calls=%async_computation.2 | async-start | bytes 23592960 | tf_op jit(solution)/shard_map/all_gather | solution.py:40
  7.3 0.8 copy-start
  7.3 10.3 %copy-start.3 = (s32[32]{0:T(128)S(1)}, s32[32]{0:T(128)}, u32[]{:S(2)}) copy-start(s32[32]{0:T(128)} %param.11) | copy-start | bytes 388
  7.3 10.4 %copy-start.1 = (s32[1024,1]{0,1:T(1,128)S(1)}, s32[1024,1]{0,1:T(1,128)}, u32[]{:S(2)}) copy-start(s32[1024,1]{0,1:T(1,128)} %param.10) | copy-start | bytes 12292
  7.3 245.2 %all-gather.5.cloned.1.call-start = ((), (), s32[]{:S(2)}) async-start(), calls=%async_computation.3 | async-start | bytes 23592960 | tf_op jit(solution)/shard_map/all_gather | solution.py:41
  8.0 19.2 %copy-start.5 = (s32[2]{0:T(128)S(1)}, s32[2]{0:T(128)}, u32[]{:S(2)}) copy-start(s32[2]{0:T(128)} %constant.40) | copy-start | bytes 28
  8.0 19.3 %copy-start.4 = (s32[2]{0:T(128)S(1)}, s32[2]{0:T(128)}, u32[]{:S(2)}) copy-start(s32[2]{0:T(128)} %constant.43) | copy-start | bytes 28
  462.7 14.3 %copy-start.2 = (f32[1024]{0:T(1024)S(1)}, f32[1024]{0:T(1024)}, u32[]{:S(2)}) copy-start(f32[1024]{0:T(1024)} %param.8) | copy-start | bytes 12292
Sparse Core Ops, SparseCore 0:
  8.9 122.6 all-gather.2
  133.2 119.2 all-gather.4
where the time goes:
time: 493 us; the launch traced here: 486 us
  blocking collectives  222 us (45%)
  waiting for transfers between devices  98.6 us (20%)
  matrix products  81.3 us (16%)
  local copies, waits for them, and re-layouts  48.2 us (10%)
  other arithmetic  21.8 us (4%)
  between operations  14.1 us (3%)
    all_to_all x1, blocking collectives, on_device(): lax.all_to_all(buffer, 'expert', split_axis=1, concat_axis=0, tiled=True)  112 us
    all_to_all x1, blocking collectives, on_device(): lax.all_to_all(result, 'expert', split_axis=0, concat_axis=1, tiled=True)  110 us
    all_gather x1, waiting for transfers between devices, on_device(): lax.all_gather(w_out, 'helper', axis=1, tiled=True)  97.2 us
    dot_general x16, matrix products, quarter_term(): return jnp.dot(hidden, weight_out, preferred_element_type=jnp.float32)  81.3 us
    another operation x6, other arithmetic  18.3 us
    gather x1, local copies, waits for them, and re-layouts, on_device(): picked = returned[slots, final]  14.3 us
    all_to_all x2, local copies, waits for them, and re-layouts, on_device(): lax.all_to_all(result, 'expert', split_axis=0, concat_axis=1, tiled=True)  13.4 us
  transfers between devices with their start and end apart: 2, of which 1 were waited for; matrix products, arithmetic and copies ran while one was open for 7% of the time, Pallas kernels for 0%

commit v1 on v0

v1 whole, which is shorter than its diff:
```python
import jax
import jax.numpy as jnp
from jax import lax
from jax.sharding import PartitionSpec as P


def ranks(onehot):
    rows = onehot.shape[0]
    earlier = lax.broadcasted_iota(jnp.int32, (rows, rows), 0) > lax.broadcasted_iota(
        jnp.int32, (rows, rows), 1
    )
    counts = jnp.dot(
        earlier.astype(jnp.bfloat16),
        onehot.astype(jnp.bfloat16),
        preferred_element_type=jnp.float32,
    )
    return jnp.sum(jnp.where(onehot, counts, 0.0), axis=1).astype(jnp.int32)


def assign(first, backup, capacity, count, slot):
    columns = jnp.arange(count, dtype=jnp.int32)
    onehot = first[:, None] == columns[None, :]
    rank = ranks(onehot)
    limit = jnp.sum(jnp.where(onehot, capacity[None, :], 0), axis=1)
    kept = rank < limit
    spill = (backup[:, None] == columns[None, :]) & ~kept[:, None]
    spill_rank = ranks(spill)
    final = jnp.where(kept, first, backup)
    slots = jnp.where(kept, rank, slot + spill_rank)
    return slots, final


def on_device(tokens, gate, expert_ids, backup_ids, capacity, w_in, w_out):
    held = w_in.shape[0]
    owners = lax.axis_size("expert")
    experts = held * owners
    rows, width = tokens.shape
    slot = max(6, 3 * rows // (2 * experts))
    room = 2 * slot

    gathered = []
    for expert in range(held):
        gathered.append(
            (
                lax.all_gather(w_in[expert], "helper", axis=1, tiled=True),
                lax.all_gather(w_out[expert], "helper", axis=0, tiled=True),
            )
        )

    slots, final = assign(expert_ids[:, 0], backup_ids[:, 0], capacity, experts, slot)
    place = (final // held) * room + slots
    which = final % held

    arrived = []
    for expert in range(held):
        target = jnp.where(which == expert, place, -1)
        hot = lax.broadcasted_iota(jnp.int32, (owners * room, rows), 0) == target[None, :]
        buffer = jnp.dot(
            hot.astype(jnp.bfloat16), tokens, preferred_element_type=jnp.float32
        ).astype(jnp.bfloat16)
        arrived.append(lax.all_to_all(buffer, "expert", split_axis=0, concat_axis=0, tiled=True))

    picked = jnp.zeros((rows, width), jnp.float32)
    for expert in range(held):
        whole_in, whole_out = gathered[expert]
        hidden = jax.nn.relu(
            jnp.dot(arrived[expert], whole_in, preferred_element_type=jnp.float32)
        ).astype(jnp.bfloat16)
        result = jnp.dot(hidden, whole_out, preferred_element_type=jnp.float32).astype(
            jnp.bfloat16
        )
        returned = lax.all_to_all(result, "expert", split_axis=0, concat_axis=0, tiled=True)
        source = jnp.where(which == expert, place, -1)
        hot = source[:, None] == lax.broadcasted_iota(jnp.int32, (rows, owners * room), 1)
        picked = picked + jnp.dot(
            hot.astype(jnp.bfloat16), returned, preferred_element_type=jnp.float32
        )
    return (gate[:, None] * picked).astype(jnp.bfloat16)


def solution(mesh):
    placed = (
        P(("expert", "helper"), None),
        P(("expert", "helper")),
        P(("expert", "helper"), None),
        P(("expert", "helper"), None),
        P(),
        P("expert", None, "helper"),
        P("expert", "helper", None),
    )
    return jax.shard_map(
        on_device,
        mesh=mesh,
        in_specs=placed,
        out_specs=P(("expert", "helper"), None),
        check_vma=False,
    )
```

time: 493 us -> 393 us (0.80)
  blocking collectives: 222 us -> 0 us
  waiting for transfers between devices: 98.6 us -> 241 us
  starting transfers between devices: 0.04 us -> 38.1 us
  local copies, waits for them, and re-layouts: 48.2 us -> 13.5 us
  other arithmetic: 21.8 us -> 0.19 us
    all_to_all x2 -> x0, blocking collectives: 222 us -> none  [the longest x1 112 us: on_device(): lax.all_to_all(buffer, 'expert', split_axis=1, concat_axis=0, tiled=True)]
    all_to_all x0 -> x8, waiting for transfers between devices: none -> 122 us  [the longest x4 93.7 us: on_device(): lax.all_to_all(buffer, 'expert', split_axis=0, concat_axis=0, tiled=True)]
    all_to_all x0 -> x8, starting transfers between devices: none -> 37.8 us  [the longest x4 19.4 us: on_device(): lax.all_to_all(result, 'expert', split_axis=0, concat_axis=0, tiled=True)]
    another operation x7 -> x0, other arithmetic: 20 us -> none
    all_gather x2 -> x8, waiting for transfers between devices: 97.2 us -> 116 us  [the longest x4 83.3 us: on_device(): lax.all_gather(w_out[expert], 'helper', axis=0, tiled=True)]
    all_to_all x3 -> x0, local copies, waits for them, and re-layouts: 15.9 us -> none  [the longest x2 13.4 us: on_device(): lax.all_to_all(result, 'expert', split_axis=0, concat_axis=1, tiled=True)]
    gather x1 -> x0, local copies, waits for them, and re-layouts: 14.3 us -> none  [on_device(): picked = returned[slots, final]]
    slice x2, local copies, waits for them, and re-layouts: 0.22 us -> 9.27 us  [the longest x1 4.65 us: on_device(): w_in[expert]]
  transfers between devices with their start and end apart: 2 -> 16, of which waited for: 1 -> 11; matrix products, arithmetic and copies ran while one was open for 7% -> 20% of each run, Pallas kernels for 0% -> 0%
where the time goes in v1:
time: 393 us; the launch traced here: 386 us
  waiting for transfers between devices  241 us (61%)
  matrix products  78.5 us (20%)
  starting transfers between devices  38.1 us (10%)
  between operations  14.1 us (4%)
  local copies, waits for them, and re-layouts  13.5 us (3%)
    all_to_all x4, waiting for transfers between devices, on_device(): lax.all_to_all(buffer, 'expert', split_axis=0, concat_axis=0, tiled=True)  93.7 us
    all_gather x4, waiting for transfers between devices, on_device(): lax.all_gather(w_out[expert], 'helper', axis=0, tiled=True)  83.3 us
    dot_general x4, matrix products, on_device(): jnp.dot(hidden, whole_out, preferred_element_type=jnp.float32)  50.6 us
    all_gather x4, waiting for transfers between devices, on_device(): lax.all_gather(w_in[expert], 'helper', axis=1, tiled=True)  32.2 us
    all_to_all x4, waiting for transfers between devices, on_device(): lax.all_to_all(result, 'expert', split_axis=0, concat_axis=0, tiled=True)  28.5 us
    all_to_all x4, starting transfers between devices, on_device(): lax.all_to_all(result, 'expert', split_axis=0, concat_axis=0, tiled=True)  19.4 us
    all_to_all x4, starting transfers between devices, on_device(): lax.all_to_all(buffer, 'expert', split_axis=0, concat_axis=0, tiled=True)  18.4 us
    dot_general x4, matrix products, on_device(): jnp.dot(hot.astype(jnp.bfloat16), returned, preferred_element_type=jnp.fl...  16.7 us
  transfers between devices with their start and end apart: 16, of which 11 were waited for; matrix products, arithmetic and copies ran while one was open for 20% of the time, Pallas kernels for 0%

profile of v1, /device:TPU:0, one launch (start us, length us, event | category | flops | bytes accessed | tf_op | source)
XLA Modules:
  0.0 385.7 jit_solution(8376530111632891269)
XLA Ops:
  6.5 4.6 %fusion.75 = (bf16[1,768,768]{2,1,0:T(8,128)(2,1)}, bf16[1,768,768]{2,1,0:T(8,128)(2,1)}, bf16[1,768,768]{2,1,0:T(8,128)(2,1)}, bf16[1,768,768]{2,1,0:T(8,128)(2,1)}) fusion(bf16[4,768,768]{2,1,0:T(8,128)(2,1)} %param.12), kind=kLoop, calls=%fused_computation.96 | loop fusion | bytes 9437184 | tf_op jit(solution)/shard_map/slice | solution.py:45
  11.3 4.6 %fusion.76 = (bf16[1,768,768]{2,1,0:T(8,128)(2,1)}, bf16[1,768,768]{2,1,0:T(8,128)(2,1)}, bf16[1,768,768]{2,1,0:T(8,128)(2,1)}, bf16[1,768,768]{2,1,0:T(8,128)(2,1)}) fusion(bf16[4,768,768]{2,1,0:T(8,128)(2,1)} %param.13), kind=kLoop, calls=%fused_computation.97 | loop fusion | bytes 9437184 | tf_op jit(solution)/shard_map/slice | solution.py:46
  23.0 7.3 %all-to-all-start = ((bf16[8,96,768]{2,1,0:T(8,128)(2,1)}), bf16[8,96,768]{2,1,0:T(8,128)(2,1)S(1)}, u32[]{:S(2)}, u32[]{:S(2)}) async-start(bf16[8,96,768]{2,1,0:T(8,128)(2,1)} %bitcast.91), calls=%async_computation | async-start | bytes 2359296 | tf_op jit(solution)/shard_map/all_to_all | solution.py:61
  32.8 26.0 %all-to-all-done = bf16[8,96,768]{2,1,0:T(8,128)(2,1)S(1)} async-done(((bf16[8,96,768]{2,1,0:T(8,128)(2,1)}), bf16[8,96,768]{2,1,0:T(8,128)(2,1)S(1)}, u32[]{:S(2)}, u32[]{:S(2)}) %all-to-all-start) | async-done | bytes 1179680 | tf_op jit(solution)/shard_map/all_to_all | solution.py:61
  66.1 26.2 %all-to-all-done.2 = bf16[8,96,768]{2,1,0:T(8,128)(2,1)S(1)} async-done(((bf16[8,96,768]{2,1,0:T(8,128)(2,1)}), bf16[8,96,768]{2,1,0:T(8,128)(2,1)S(1)}, u32[]{:S(2)}, u32[]{:S(2)}) %all-to-all-start.2) | async-done | bytes 1179680 | tf_op jit(solution)/shard_map/all_to_all | solution.py:61
  100.2 25.5 %all-to-all-done.4 = bf16[8,96,768]{2,1,0:T(8,128)(2,1)S(1)} async-done(((bf16[8,96,768]{2,1,0:T(8,128)(2,1)}), bf16[8,96,768]{2,1,0:T(8,128)(2,1)S(1)}, u32[]{:S(2)}, u32[]{:S(2)}) %all-to-all-start.4) | async-done | bytes 1179680 | tf_op jit(solution)/shard_map/all_to_all | solution.py:61
  125.7 3.8 all-to-all-start.6
  129.6 12.7 %fusion.34 = bf16[768,768]{1,0:T(8,128)(2,1)} fusion(bf16[1,3072,768]{2,1,0:T(8,128)(2,1)} %all-gather.19.cloned.1.call-done, bf16[768,768]{1,0:T(8,128)(2,1)} %bitcast.82, bf16[1,768,3072]{2,1,0:T(8,128)(2,1)} %all-gather.17.cloned.1.call-done), kind=kOutput, calls=%fused_computation.48 | convolution fusion | flops 7253065728 | bytes 11796480 | tf_op jit(solution)/shard_map/dot_general | solution.py:69
  142.3 15.9 %all-to-all-done.6 = bf16[8,96,768]{2,1,0:T(8,128)(2,1)S(1)} async-done(((bf16[8,96,768]{2,1,0:T(8,128)(2,1)}), bf16[8,96,768]{2,1,0:T(8,128)(2,1)S(1)}, u32[]{:S(2)}, u32[]{:S(2)}) %all-to-all-start.6) | async-done | bytes 1179680 | tf_op jit(solution)/shard_map/all_to_all | solution.py:61
  163.0 5.4 %all-gather.23.cloned.1.call-done = bf16[1,3072,768]{2,1,0:T(8,128)(2,1)} async-done(((bf16[1,768,768]{2,1,0:T(8,128)(2,1)}), bf16[1,3072,768]{2,1,0:T(8,128)(2,1)}) %all-gather.23.cloned.1.call-update) | async-done | bytes 4718608 | tf_op jit(solution)/shard_map/all_gather | solution.py:46
  168.5 12.8 %fusion.37 = bf16[768,768]{1,0:T(8,128)(2,1)} fusion(bf16[1,3072,768]{2,1,0:T(8,128)(2,1)} %all-gather.23.cloned.1.call-done, bf16[768,768]{1,0:T(8,128)(2,1)} %bitcast.81, bf16[1,768,3072]{2,1,0:T(8,128)(2,1)} %all-gather.21.cloned.1.call-done), kind=kOutput, calls=%fused_computation.49 | convolution fusion | flops 7253065728 | bytes 11796480 | tf_op jit(solution)/shard_map/dot_general | solution.py:69
  181.2 10.6 %all-to-all-done.1 = bf16[8,96,768]{2,1,0:T(8,128)(2,1)S(1)} async-done(((bf16[8,96,768]{2,1,0:T(8,128)(2,1)}), bf16[8,96,768]{2,1,0:T(8,128)(2,1)S(1)}, u32[]{:S(2)}, u32[]{:S(2)}) %all-to-all-start.1) | async-done | bytes 1179680 | tf_op jit(solution)/shard_map/all_to_all | solution.py:72
  191.8 4.5 %all-to-all-start.3 = ((bf16[8,96,768]{2,1,0:T(8,128)(2,1)}), bf16[8,96,768]{2,1,0:T(8,128)(2,1)}, u32[]{:S(2)}, u32[]{:S(2)}) async-start(bf16[8,96,768]{2,1,0:T(8,128)(2,1)} %bitcast.86), calls=%async_computation.3 | async-start | bytes 2359296 | tf_op jit(solution)/shard_map/all_to_all | solution.py:72
  196.2 11.1 %all-gather.25.cloned.1.call-done = bf16[1,768,3072]{2,1,0:T(8,128)(2,1)} async-done(((bf16[1,768,768]{2,1,0:T(8,128)(2,1)}), bf16[1,768,3072]{2,1,0:T(8,128)(2,1)}) %all-gather.25.cloned.1.call-update) | async-done | bytes 4718608 | tf_op jit(solution)/shard_map/all_gather | solution.py:45
  207.3 38.9 %all-gather.27.cloned.1.call-done = bf16[1,3072,768]{2,1,0:T(8,128)(2,1)} async-done(((bf16[1,768,768]{2,1,0:T(8,128)(2,1)}), bf16[1,3072,768]{2,1,0:T(8,128)(2,1)}) %all-gather.27.cloned.1.call-update) | async-done | bytes 4718608 | tf_op jit(solution)/shard_map/all_gather | solution.py:46
  246.2 12.4 %fusion.40 = bf16[768,768]{1,0:T(8,128)(2,1)} fusion(bf16[1,3072,768]{2,1,0:T(8,128)(2,1)} %all-gather.27.cloned.1.call-done, bf16[768,768]{1,0:T(8,128)(2,1)S(1)} %bitcast.79, bf16[1,768,3072]{2,1,0:T(8,128)(2,1)} %all-gather.25.cloned.1.call-done), kind=kOutput, calls=%fused_computation.50 | convolution fusion | flops 7253065728 | bytes 11796480 | tf_op jit(solution)/shard_map/dot_general | solution.py:69
  258.6 5.5 %all-to-all-start.5 = ((bf16[8,96,768]{2,1,0:T(8,128)(2,1)}), bf16[8,96,768]{2,1,0:T(8,128)(2,1)S(1)}, u32[]{:S(2)}, u32[]{:S(2)}) async-start(bf16[8,96,768]{2,1,0:T(8,128)(2,1)} %bitcast.87), calls=%async_computation.5 | async-start | bytes 2359296 | tf_op jit(solution)/shard_map/all_to_all | solution.py:72
  264.2 21.1 %all-gather.29.cloned.1.call-done = bf16[1,768,3072]{2,1,0:T(8,128)(2,1)} async-done(((bf16[1,768,768]{2,1,0:T(8,128)(2,1)}), bf16[1,768,3072]{2,1,0:T(8,128)(2,1)}) %all-gather.29.cloned.1.call-update) | async-done | bytes 4718608 | tf_op jit(solution)/shard_map/all_gather | solution.py:45
  285.3 39.0 %all-gather.31.cloned.1.call-done = bf16[1,3072,768]{2,1,0:T(8,128)(2,1)} async-done(((bf16[1,768,768]{2,1,0:T(8,128)(2,1)}), bf16[1,3072,768]{2,1,0:T(8,128)(2,1)}) %all-gather.31.cloned.1.call-update) | async-done | bytes 4718608 | tf_op jit(solution)/shard_map/all_gather | solution.py:46
  324.3 12.7 %fusion.43 = bf16[768,768]{1,0:T(8,128)(2,1)} fusion(bf16[1,3072,768]{2,1,0:T(8,128)(2,1)} %all-gather.31.cloned.1.call-done, bf16[768,768]{1,0:T(8,128)(2,1)} %bitcast.80, bf16[1,768,3072]{2,1,0:T(8,128)(2,1)} %all-gather.29.cloned.1.call-done), kind=kOutput, calls=%fused_computation.51 | convolution fusion | flops 7253065728 | bytes 11796480 | tf_op jit(solution)/shard_map/dot_general | solution.py:69
  338.0 5.8 %all-to-all-start.7 = ((bf16[8,96,768]{2,1,0:T(8,128)(2,1)}), bf16[8,96,768]{2,1,0:T(8,128)(2,1)S(1)}, u32[]{:S(2)}, u32[]{:S(2)}) async-start(bf16[8,96,768]{2,1,0:T(8,128)(2,1)} %bitcast.84), calls=%async_computation.7 | async-start | bytes 2359296 | tf_op jit(solution)/shard_map/all_to_all | solution.py:72
  347.1 4.6 %fusion.16 = f32[1024,768]{1,0:T(8,128)} fusion(bf16[768,768]{1,0:T(8,128)(2,1)} %bitcast.18, s32[1024]{0:T(1024)S(1)} %bitcast.102), kind=kOutput, calls=%fused_computation.30 | convolution fusion | flops 1208745984 | bytes 4329472 | tf_op jit(solution)/shard_map/dot_general | solution.py:75
  354.9 17.9 %all-to-all-done.7 = bf16[8,96,768]{2,1,0:T(8,128)(2,1)S(1)} async-done(((bf16[8,96,768]{2,1,0:T(8,128)(2,1)}), bf16[8,96,768]{2,1,0:T(8,128)(2,1)S(1)}, u32[]{:S(2)}, u32[]{:S(2)}) %all-to-all-start.7) | async-done | bytes 1179680 | tf_op jit(solution)/shard_map/all_to_all | solution.py:72
  372.7 5.7 %multiply_convert_fusion = bf16[1024,768]{1,0:T(8,128)(2,1)} fusion(f32[1024,768]{1,0:T(8,128)} %fusion.18, f32[1024,768]{1,0:T(8,128)} %fusion.14, f32[1024,768]{1,0:T(8,128)} %fusion.16, f32[1024]{0:T(1024)S(1)} %copy-done.9, bf16[768,768]{1,0:T(8,128)(2,1)S(1)} %bitcast.77, s32[1024]{0:T(1024)S(1)} %bitcast.96), kind=kOutput, calls=%fused_computation.19 | convolution fusion | flops 1212678144 | bytes 12197888 | tf_op jit(solution)/shard_map/dot_general | solution.py:75
  (61 shorter events, 36.9 us)
Async XLA Ops:
  6.5 13.9 %copy-start = (bf16[1024,768]{1,0:T(8,128)(2,1)S(1)}, bf16[1024,768]{1,0:T(8,128)(2,1)}, u32[]{:S(2)}) copy-start(bf16[1024,768]{1,0:T(8,128)(2,1)} %param.7) | copy-start | bytes 4718596
  6.5 123.1 %all-gather.17.cloned.1.call-start = ((), (), s32[]{:S(2)}) async-start(), calls=%async_computation.8 | async-start | bytes 5898240 | tf_op jit(solution)/shard_map/all_gather | solution.py:45
  11.2 118.4 %all-gather.19.cloned.1.call-start = ((), (), s32[]{:S(2)}) async-start(), calls=%async_computation.9 | async-start | bytes 5898240 | tf_op jit(solution)/shard_map/all_gather | solution.py:46
  15.9 3.3 copy-start.7
  15.9 147.1 %all-gather.21.cloned.1.call-start = ((), (), s32[]{:S(2)}) async-start(), calls=%async_computation.10 | async-start | bytes 5898240 | tf_op jit(solution)/shard_map/all_gather | solution.py:45
  16.7 3.1 copy-start.10
  16.7 3.2 copy-start.8
  16.7 151.8 %all-gather.23.cloned.1.call-start = ((), (), s32[]{:S(2)}) async-start(), calls=%async_computation.11 | async-start | bytes 5898240 | tf_op jit(solution)/shard_map/all_gather | solution.py:46
  17.3 190.1 %all-gather.25.cloned.1.call-start = ((), (), s32[]{:S(2)}) async-start(), calls=%async_computation.12 | async-start | bytes 5898240 | tf_op jit(solution)/shard_map/all_gather | solution.py:45
  17.8 228.4 %all-gather.27.cloned.1.call-start = ((), (), s32[]{:S(2)}) async-start(), calls=%async_computation.13 | async-start | bytes 5898240 | tf_op jit(solution)/shard_map/all_gather | solution.py:46
  18.4 266.8 %all-gather.29.cloned.1.call-start = ((), (), s32[]{:S(2)}) async-start(), calls=%async_computation.14 | async-start | bytes 5898240 | tf_op jit(solution)/shard_map/all_gather | solution.py:45
  23.0 35.9 %all-to-all-start = ((bf16[8,96,768]{2,1,0:T(8,128)(2,1)}), bf16[8,96,768]{2,1,0:T(8,128)(2,1)S(1)}, u32[]{:S(2)}, u32[]{:S(2)}) async-start(bf16[8,96,768]{2,1,0:T(8,128)(2,1)} %bitcast.91), calls=%async_computation | async-start | bytes 2359296 | tf_op jit(solution)/shard_map/all_to_all | solution.py:61
  59.9 32.4 %all-to-all-start.2 = ((bf16[8,96,768]{2,1,0:T(8,128)(2,1)}), bf16[8,96,768]{2,1,0:T(8,128)(2,1)S(1)}, u32[]{:S(2)}, u32[]{:S(2)}) async-start(bf16[8,96,768]{2,1,0:T(8,128)(2,1)} %bitcast.90), calls=%async_computation.2 | async-start | bytes 2359296 | tf_op jit(solution)/shard_map/all_to_all | solution.py:61
  93.3 32.4 %all-to-all-start.4 = ((bf16[8,96,768]{2,1,0:T(8,128)(2,1)}), bf16[8,96,768]{2,1,0:T(8,128)(2,1)S(1)}, u32[]{:S(2)}, u32[]{:S(2)}) async-start(bf16[8,96,768]{2,1,0:T(8,128)(2,1)} %bitcast.88), calls=%async_computation.4 | async-start | bytes 2359296 | tf_op jit(solution)/shard_map/all_to_all | solution.py:61
  97.0 227.3 %all-gather.31.cloned.1.call-start = ((), (), s32[]{:S(2)}) async-start(), calls=%async_computation.15 | async-start | bytes 5898240 | tf_op jit(solution)/shard_map/all_gather | solution.py:46
  125.7 32.5 %all-to-all-start.6 = ((bf16[8,96,768]{2,1,0:T(8,128)(2,1)}), bf16[8,96,768]{2,1,0:T(8,128)(2,1)S(1)}, u32[]{:S(2)}, u32[]{:S(2)}) async-start(bf16[8,96,768]{2,1,0:T(8,128)(2,1)} %bitcast.89), calls=%async_computation.6 | async-start | bytes 2359296 | tf_op jit(solution)/shard_map/all_to_all | solution.py:61
  158.3 1.1 copy-start.2
  159.4 32.4 %all-to-all-start.1 = ((bf16[8,96,768]{2,1,0:T(8,128)(2,1)}), bf16[8,96,768]{2,1,0:T(8,128)(2,1)S(1)}, u32[]{:S(2)}, u32[]{:S(2)}) async-start(bf16[8,96,768]{2,1,0:T(8,128)(2,1)} %bitcast.85), calls=%async_computation.1 | async-start | bytes 2359296 | tf_op jit(solution)/shard_map/all_to_all | solution.py:72
  191.8 66.9 %all-to-all-start.3 = ((bf16[8,96,768]{2,1,0:T(8,128)(2,1)}), bf16[8,96,768]{2,1,0:T(8,128)(2,1)}, u32[]{:S(2)}, u32[]{:S(2)}) async-start(bf16[8,96,768]{2,1,0:T(8,128)(2,1)} %bitcast.86), calls=%async_computation.3 | async-start | bytes 2359296 | tf_op jit(solution)/shard_map/all_to_all | solution.py:72
  258.6 78.4 %all-to-all-start.5 = ((bf16[8,96,768]{2,1,0:T(8,128)(2,1)}), bf16[8,96,768]{2,1,0:T(8,128)(2,1)S(1)}, u32[]{:S(2)}, u32[]{:S(2)}) async-start(bf16[8,96,768]{2,1,0:T(8,128)(2,1)} %bitcast.87), calls=%async_computation.5 | async-start | bytes 2359296 | tf_op jit(solution)/shard_map/all_to_all | solution.py:72
  338.0 34.7 %all-to-all-start.7 = ((bf16[8,96,768]{2,1,0:T(8,128)(2,1)}), bf16[8,96,768]{2,1,0:T(8,128)(2,1)S(1)}, u32[]{:S(2)}, u32[]{:S(2)}) async-start(bf16[8,96,768]{2,1,0:T(8,128)(2,1)} %bitcast.84), calls=%async_computation.7 | async-start | bytes 2359296 | tf_op jit(solution)/shard_map/all_to_all | solution.py:72
  347.1 4.6 %copy-start.6 = (bf16[8,96,768]{2,1,0:T(8,128)(2,1)S(1)}, bf16[8,96,768]{2,1,0:T(8,128)(2,1)}, u32[]{:S(2)}) copy-start(bf16[8,96,768]{2,1,0:T(8,128)(2,1)} %copy-done.5) | copy-start | bytes 3538948
  351.6 21.1 %copy-start.9 = (f32[1024]{0:T(1024)S(1)}, f32[1024]{0:T(1024)}, u32[]{:S(2)}) copy-start(f32[1024]{0:T(1024)} %param.8) | copy-start | bytes 12292
  372.7 5.7 %copy-start.1 = (bf16[1024,768]{1,0:T(8,128)(2,1)S(1)}, bf16[1024,768]{1,0:T(8,128)(2,1)}, u32[]{:S(2)}) copy-start(bf16[1024,768]{1,0:T(8,128)(2,1)} %param.7) | copy-start | bytes 4718596
  (3 other events, 3.1 us)
Sparse Core Ops, SparseCore 0:
  11.3 40.1 all-gather.16
  53.1 37.4 all-gather.18
  92.1 37.4 all-gather.20
  131.0 37.4 all-gather.22
  169.9 37.4 all-gather.24
  208.8 37.4 all-gather.26
  247.8 37.4 all-gather.28
  286.8 37.4 all-gather.30
